TPU v7x, 32 devices: a whole 2x2x4 slice. The times are simulated.
32 devices in a mesh: seq: 8 (over y, x, core), head: 4 (over z).
Axes of the slice: x: 2, y: 2, z: 4, core: 2. Of those that a mesh axis runs over, the one named last changes fastest.
Arguments:
- latent: bfloat16 [1024, 1024], P('seq'), may hold values from -15 to 15
- probe: bfloat16 [1024, 1024], P('seq'), may hold values from -6 to 6
- time_embed: float32 [1024], replicated, may hold values from -6 to 6
- gain_attn: float32 [1024], replicated, may hold values from 0.1 to 1.9
- w_query: bfloat16 [1024, 1024], P(None, 'head'), may hold values from -0.625 to 0.625
- w_key: bfloat16 [1024, 1024], P(None, 'head'), may hold values from -11 to 11
- w_value: bfloat16 [1024, 1024], P(None, 'head'), may hold values from -0.1875 to 0.1875
- w_out: bfloat16 [1024, 1024], P('head'), may hold values from -0.1875 to 0.1875
- gain_mlp: float32 [1024], replicated, may hold values from 0.1 to 1.9
- w_in: bfloat16 [1024, 4096], P(None, 'head'), may hold values from -0.1875 to 0.1875
- w_down: bfloat16 [4096, 1024], P('head'), may hold values from -0.09375 to 0.09375
Outputs:
- latent_end: float32 [1024, 1024], P('seq')
- frame_trace: float32 [1024], P('seq')
- frame_logp: float32 [1024], P('seq')
- mean_logp: float32 [], replicated
All inputs are finite; a program needn't handle non-finite values.
Results may differ from a plain program's by a relative error of at most 0.03.
The roundings to bfloat16 on the way count: a program that leaves them out, or rounds other values in their place, can miss the bound.
Values may be sent and summed in bfloat16 or wider, within the bound.
A program may use at most 64 MiB of HBM per device.

v0:
```python
import functools
import math

import jax
import jax.numpy as jnp
from jax import lax
from jax.experimental import pallas as pl
from jax.experimental.pallas import tpu as pltpu
from jax.sharding import PartitionSpec as P

HEAD_DIM = 64
STEPS = 2
EPSILON = 1e-05
GELU_COEF = 0.044715
ROOT_TWO_PI = math.sqrt(2.0 / math.pi)
LANES = 128
HALVES = 2
BF16 = jnp.bfloat16
F32 = jnp.float32


def norm_pair(values, tangent, norm_gain):
    meansq = jnp.mean(values * values, axis=-1, keepdims=True) + EPSILON
    inverse = lax.rsqrt(meansq)
    inner_mean = jnp.mean(values * tangent, axis=-1, keepdims=True)
    primal = values * inverse * norm_gain
    derived = (tangent * inverse - values * (inverse * inverse * inverse * inner_mean)) * norm_gain
    return (primal.astype(BF16), derived.astype(BF16))


def gelu_pair(pre_act, tangent):
    square = pre_act * pre_act
    tanh_value = jnp.tanh(ROOT_TWO_PI * pre_act * (1.0 + GELU_COEF * square))
    half = 0.5 * (1.0 + tanh_value)
    slope_value = half + 0.5 * pre_act * (1.0 - tanh_value * tanh_value) * (
        ROOT_TWO_PI * (1.0 + 3.0 * GELU_COEF * square)
    )
    return ((pre_act * half).astype(BF16), (slope_value * tangent).astype(BF16))


def dot(a, b):
    return jnp.dot(a, b, preferred_element_type=F32)


def dot_t(a, b):
    return lax.dot_general(a, b, (((1,), (1,)), ((), ())), preferred_element_type=F32)


def flow_kernel(
    n,
    m,
    latent,
    probe,
    time_embed,
    gain_attn,
    gain_mlp,
    w_query,
    w_key,
    w_value,
    w_out,
    w_in,
    w_down,
    latent_end,
    stats_out,
    mean_out,
    wqkv,
    wout,
    win,
    wdown,
    normed,
    qbuf,
    kbuf,
    vbuf,
    headall,
    inbuf,
    probe_down,
    partial,
    rssend,
    rsrecv,
    state,
    delta,
    tracebuf,
    tilebuf,
    sumbuf,
    wsem,
    wsend,
    wrecv,
    kvsend,
    kvrecv,
    zsend,
    zrecv,
    ssend,
    srecv,
    msend,
    mrecv,
):
    s = lax.axis_index("seq")
    z = lax.axis_index("head")
    rows, width = latent.shape
    hrows = rows // HALVES
    part = hrows // m
    cols = w_query.shape[1]
    pairs = cols // LANES

    def flip(bit):
        return s + bit - 2 * bit * lax.rem(s // bit, 2)

    def zpeer(d):
        return lax.rem(z + d, m)

    def zfrom(d):
        return lax.rem(z + m - d, m)

    def remote(src, dst, send, recv, target_s, target_z):
        return pltpu.make_async_remote_copy(
            src_ref=src,
            dst_ref=dst,
            send_sem=send,
            recv_sem=recv,
            device_id=(target_s, target_z),
            device_id_type=pl.DeviceIdType.MESH,
        )

    loads = [
        pltpu.make_async_copy(w_query, wqkv.at[:, pl.ds(0, cols)], wsem.at[0]),
        pltpu.make_async_copy(w_key, wqkv.at[:, pl.ds(cols, cols)], wsem.at[1]),
        pltpu.make_async_copy(w_value, wqkv.at[:, pl.ds(2 * cols, cols)], wsem.at[2]),
        pltpu.make_async_copy(w_out, wout.at[z], wsem.at[3]),
        pltpu.make_async_copy(w_in, win, wsem.at[4]),
        pltpu.make_async_copy(w_down, wdown, wsem.at[5]),
    ]
    for index in (1, 2, 3, 0, 5, 4):
        loads[index].start()

    barrier = pltpu.get_barrier_semaphore()
    for d in range(1, m):
        pl.semaphore_signal(
            barrier, inc=1, device_id=(s, zpeer(d)), device_id_type=pl.DeviceIdType.MESH
        )
    for d in range(1, n):
        pl.semaphore_signal(
            barrier,
            inc=1,
            device_id=(lax.rem(s + d, n), z),
            device_id_type=pl.DeviceIdType.MESH,
        )

    def own_rows(h):
        return pl.ds(pl.multiple_of(h * hrows + z * part, part), part)

    def norm_all():
        for h in range(HALVES):
            span = slice(h * hrows, (h + 1) * hrows)
            prim, tang = norm_pair(inbuf[span, :], probe[span, :].astype(F32), gain_attn[...])
            normed[span, :] = prim
            normed[rows + h * hrows : rows + (h + 1) * hrows, :] = tang

    inbuf[...] = latent[...].astype(F32)
    norm_all()
    for h in range(HALVES):
        state[h] = latent[own_rows(h), :].astype(F32)

    pl.semaphore_wait(barrier, n + m - 2)

    half = cols // 2
    core = lax.rem(s, 2)
    mine = pl.ds(pl.multiple_of(core * half, half), half)
    quarter = half // 2
    turn = lax.rem(s // 2, 2) * (1 - core) + lax.rem(s // 4, 2) * core
    buddy = flip(2) * (1 - core) + flip(4) * core
    fetched = pl.ds(pl.multiple_of(core * half + turn * quarter, quarter), quarter)
    partner = flip(1)
    loads[3].wait()
    w_copies = []
    for d in range(1, m):
        copy = remote(
            wout.at[z, fetched], wout.at[z, fetched], wsend.at[0, d], wrecv.at[0, d], s, zpeer(d)
        )
        copy.start()
        w_copies.append(copy)

    def kv_exchange(k, p):
        bufs = (kbuf, vbuf)
        sends = []

        def give(which, slot, target, at):
            copy = remote(
                bufs[which].at[k, p, slot],
                bufs[which].at[k, p, slot],
                kvsend.at[k, p, len(sends)],
                kvrecv.at[k, p, which, at],
                target,
                z,
            )
            copy.start()
            sends.append(copy)

        def got(which, slot, at):
            pltpu.make_async_copy(
                bufs[which].at[k, p, slot], bufs[which].at[k, p, slot], kvrecv.at[k, p, which, at]
            ).wait()

        xn, yn = flip(2), flip(4)
        dn = yn + 2 - 4 * lax.rem(yn // 2, 2)

        def own(which):
            if n == 8:
                first, second = ((xn, 2), (yn, 4)) if which == 0 else ((yn, 4), (xn, 2))
                give(which, s, *first)
                give(which, s, *second)
                give(which, s, partner, 1)
            else:
                for d in range(1, n):
                    give(which, s, lax.rem(s + d, n), d)

        def relay():
            if n == 8:
                got(0, xn, 2)
                give(0, xn, yn, 6)
                got(1, yn, 4)
                give(1, yn, xn, 6)
                give(0, xn, partner, 3)
                give(1, yn, partner, 5)

        def rest():
            if n == 8:
                got(0, yn, 4)
                give(0, yn, partner, 5)
                got(1, xn, 2)
                give(1, xn, partner, 3)
                got(0, dn, 6)
                give(0, dn, partner, 7)
                got(1, dn, 6)
                give(1, dn, partner, 7)
                slots = ((s, 1), (xn, 3), (yn, 5), (dn, 7))
                for which in range(2):
                    for slot, at in slots:
                        got(which, slot + 1 - 2 * lax.rem(slot, 2), at)
            else:
                for which in range(2):
                    for d in range(1, n):
                        got(which, lax.rem(s + n - d, n), d)

        return sends, own, relay, rest

    lane = lax.broadcasted_iota(jnp.int32, (1, LANES), 1)
    scale = HEAD_DIM ** (-0.5)
    frames = rows * n
    trace = [None] * HALVES

    for k in range(STEPS):

        def project(which):
            if k == 0:
                loads[which].wait()
            weight = wqkv[:, which * cols : (which + 1) * cols]
            return dot(normed[...], weight).astype(BF16).reshape(2, rows, cols)

        def z_start(phase, src_of, dst):
            copies = []
            for d in range(m - 1, 0, -1):
                copy = remote(
                    src_of(zpeer(d)),
                    dst,
                    zsend.at[k, phase, d],
                    zrecv.at[k, phase, d],
                    s,
                    zpeer(d),
                )
                copy.start()
                copies.append(copy)
            return copies

        def z_wait(copies):
            for copy in copies:
                copy.wait_send()
                copy.wait_recv()

        exchanges = [kv_exchange(k, p) for p in range(pairs)]

        def keep_pairs(ref, both):
            for p in range(pairs):
                ref[k, p, s] = both[:, :, p * LANES : (p + 1) * LANES]

        keep_pairs(kbuf, project(1))
        exchanges[0][1](0)
        keep_pairs(vbuf, project(2))
        exchanges[0][1](1)
        qbuf[...] = project(0)
        exchanges[0][2]()
        for p in range(1, pairs):
            exchanges[p][1](0)
            exchanges[p][1](1)
        if k == 0:
            loads[5].wait()
            probe_down[...] = dot_t(probe[...], wdown[...])

        def w_pass(stage, which, target):
            copies = []
            for d in range(1, m):
                copy = remote(
                    wout.at[zfrom(d), which],
                    wout.at[zfrom(d), which],
                    wsend.at[stage, d],
                    wrecv.at[stage, d],
                    target,
                    z,
                )
                copy.start()
                copies.append(copy)
            return copies

        head_copies = [[] for _ in range(HALVES)]
        for p in range(pairs):
            if k == 0 and p == pairs - 1:
                z_wait(w_copies)
                w_trades = w_pass(1, fetched, buddy)
            exchanges[p][3]()
            for h in range(HALVES):
                span = slice(h * hrows, (h + 1) * hrows)
                at = slice(p * LANES, (p + 1) * LANES)
                keys = kbuf[k, p, :, 0].reshape(frames, LANES)
                key_tang = kbuf[k, p, :, 1].reshape(frames, LANES)
                vals = vbuf[k, p, :, 0].reshape(frames, LANES)
                val_tang = vbuf[k, p, :, 1].reshape(frames, LANES)
                both_keys = jnp.concatenate([keys, key_tang], axis=1)
                both_vals = jnp.concatenate([vals, val_tang], axis=1)
                queries = qbuf[0, span, at]
                query_tang = qbuf[1, span, at]
                zero = jnp.zeros_like(queries)
                left = []
                for side in range(LANES // HEAD_DIM):
                    keep = (lane // HEAD_DIM) == side
                    q = jnp.where(keep, queries, zero)
                    qt = jnp.where(keep, query_tang, zero)
                    left.append(
                        (
                            jnp.concatenate([q, zero], axis=1),
                            jnp.concatenate([qt, q], axis=1),
                        )
                    )
                stack = [item[0] for item in left] + [item[1] for item in left]
                both = dot_t(jnp.concatenate(stack, axis=0), both_keys) * scale
                scores, score_tang = both[: 2 * hrows], both[2 * hrows :]
                weights = jnp.exp(scores - jnp.max(scores, axis=-1, keepdims=True))
                weighted = weights * score_tang
                total = jnp.sum(weights, axis=-1, keepdims=True)
                carried = jnp.sum(weighted, axis=-1, keepdims=True)
                rounded = jnp.concatenate([weights.astype(BF16), weighted.astype(BF16)], axis=0)
                mixed = dot(rounded, both_vals)
                prim = mixed[: 2 * hrows, :LANES] / total
                tang = (mixed[2 * hrows :, :LANES] + mixed[: 2 * hrows, LANES:]) / total - (
                    carried / total
                ) * prim
                first = (lane // HEAD_DIM) == 0
                headall[k, h, p, z, 0] = jnp.where(first, prim[:hrows], prim[hrows:]).astype(
                    BF16
                )
                headall[k, h, p, z, 1] = jnp.where(first, tang[:hrows], tang[hrows:]).astype(
                    BF16
                )

                head_copies[h] += z_start(
                    p * HALVES + h, lambda j: headall.at[k, h, p, z], headall.at[k, h, p, z]
                )
                if h == 0 and p + 1 < pairs:
                    exchanges[p + 1][2]()

        if k == 0:
            z_wait(w_trades)
            forwards = w_pass(2, mine, partner)
            loads[4].wait()
            z_wait(forwards)

        rs_copies = []
        for h in range(HALVES):
            span = slice(h * hrows, (h + 1) * hrows)
            z_wait(head_copies[h])
            heads = [
                headall[k, h, p, j].reshape(2 * hrows, LANES) for j in range(m) for p in range(pairs)
            ]
            attn_both = dot(jnp.concatenate(heads, axis=1), wout[...].reshape(m * cols, width))
            attn, attn_tang = attn_both[:hrows], attn_both[hrows:]
            direction = probe[span, :].astype(F32)
            pair = norm_pair(inbuf[span, :] + attn, direction + attn_tang, gain_mlp[...])
            pre = dot(jnp.concatenate(pair, axis=0), win[...])
            act, act_tang = gelu_pair(pre[:hrows], pre[hrows:])
            terms = dot(act, wdown[...])
            rssend[k, h] = terms.astype(BF16).reshape(m, part, width)
            rs_copies.append(
                z_start(pairs * HALVES + h, lambda j: rssend.at[k, h, j], rsrecv.at[k, h, z])
            )
            partial[h] = (attn + terms).reshape(m, part, width)
            grown = jnp.sum(direction * attn_tang, axis=-1, keepdims=True) / m + jnp.sum(
                act_tang.astype(F32) * probe_down[span, :], axis=-1, keepdims=True
            )
            trace[h] = grown if k == 0 else trace[h] + grown

        last = k == STEPS - 1
        if last:
            column = jnp.concatenate(trace, axis=0) / (STEPS * width)
            trace_sum = jnp.sum(column, axis=0, keepdims=True)
            tracebuf[z] = jnp.transpose(jnp.broadcast_to(column, (rows, LANES)))[:8, :]
            trace_copies = []
            for d in range(1, m):
                copy = remote(
                    tracebuf.at[z], tracebuf.at[z], ssend.at[0, d], srecv.at[0, d], s, zpeer(d)
                )
                copy.start()
                trace_copies.append(copy)

        delta_copies = []
        squares = jnp.zeros((1, 1), F32)
        for h in range(HALVES):
            z_wait(rs_copies[h])
            field = partial[h, z]
            for d in range(1, m):
                field = field + rsrecv[k, h, zfrom(d)].astype(F32)
            new_state = state[h] + field / STEPS
            state[h] = new_state
            delta[k, h, z] = (new_state - latent[own_rows(h), :].astype(F32)).astype(BF16)
            delta_copies.append(
                z_start((pairs + 1) * HALVES + h, lambda j: delta.at[k, h, z], delta.at[k, h, z])
            )
            if last:
                by_row = jnp.sum(new_state * new_state, axis=-1, keepdims=True)
                squares = squares + jnp.sum(by_row, axis=0, keepdims=True)
        for exchange in exchanges:
            for send in exchange[0]:
                send.wait_send()
        if last:
            share = trace_sum - 0.5 * squares / width
            tilebuf[z] = jnp.broadcast_to(share, (8, LANES))
            tile_copies = []
            for d in range(1, m):
                copy = remote(
                    tilebuf.at[z], tilebuf.at[z], ssend.at[1, d], srecv.at[1, d], s, zpeer(d)
                )
                copy.start()
                tile_copies.append(copy)
            z_wait(trace_copies)
            trace_row = jnp.sum(tracebuf[...], axis=0)
            z_wait(tile_copies)
            sumbuf[s] = jnp.sum(tilebuf[...], axis=0)
            mean_copies = []
            for d in range(1, n):
                copy = remote(
                    sumbuf.at[s], sumbuf.at[s], msend.at[d], mrecv.at[d], lax.rem(s + d, n), z
                )
                copy.start()
                mean_copies.append(copy)
        norms = []
        for h in range(HALVES):
            span = slice(h * hrows, (h + 1) * hrows)
            z_wait(delta_copies[h])
            following = latent[span, :].astype(F32) + delta[k, h].reshape(hrows, width).astype(F32)
            if last:
                latent_end[span, :] = following
                norms.append(jnp.sum(following * following, axis=-1, keepdims=True))
            else:
                following = following + ((k + 1) / STEPS) * time_embed[...]
                inbuf[span, :] = following
                prim, tang = norm_pair(following, probe[span, :].astype(F32), gain_attn[...])
                normed[span, :] = prim
                normed[rows + h * hrows : rows + (h + 1) * hrows, :] = tang
    norm_row = jnp.transpose(jnp.broadcast_to(jnp.concatenate(norms, axis=0), (rows, LANES)))[:8]
    half_log = 0.5 * math.log(2.0 * math.pi)
    first_row = lax.broadcasted_iota(jnp.int32, (8, rows), 0) == 0
    stats_out[...] = jnp.where(
        first_row, trace_row, trace_row - 0.5 * norm_row / width - half_log
    )
    z_wait(mean_copies)
    mean_out[...] = jnp.sum(sumbuf[...], axis=0) / frames - half_log


def per_device(
    n,
    m,
    latent,
    probe,
    time_embed,
    gain_attn,
    w_query,
    w_key,
    w_value,
    w_out,
    gain_mlp,
    w_in,
    w_down,
):
    rows, width = latent.shape
    cols = w_query.shape[1]
    hidden = w_in.shape[1]
    hrows = rows // HALVES
    part = hrows // m
    pairs = cols // LANES
    vmem = pl.BlockSpec(memory_space=pltpu.VMEM)
    anyspace = pl.BlockSpec(memory_space=pl.ANY)
    dma = pltpu.SemaphoreType.DMA
    state, stats, mean = pl.pallas_call(
        functools.partial(flow_kernel, n, m),
        out_shape=(
            jax.ShapeDtypeStruct((rows, width), F32),
            jax.ShapeDtypeStruct((8, rows), F32),
            jax.ShapeDtypeStruct((8, LANES), F32),
        ),
        in_specs=[vmem] * 5 + [anyspace] * 6,
        out_specs=(vmem, vmem, vmem),
        scratch_shapes=[
            pltpu.VMEM((width, 3 * cols), BF16),
            pltpu.VMEM((m, cols, width), BF16),
            pltpu.VMEM((width, hidden), BF16),
            pltpu.VMEM((hidden, width), BF16),
            pltpu.VMEM((2 * rows, width), BF16),
            pltpu.VMEM((2, rows, cols), BF16),
            pltpu.VMEM((STEPS, pairs, n, 2, rows, LANES), BF16),
            pltpu.VMEM((STEPS, pairs, n, 2, rows, LANES), BF16),
            pltpu.VMEM((STEPS, HALVES, pairs, m, 2, hrows, LANES), BF16),
            pltpu.VMEM((rows, width), F32),
            pltpu.VMEM((rows, hidden), F32),
            pltpu.VMEM((HALVES, m, part, width), F32),
            pltpu.VMEM((STEPS, HALVES, m, part, width), BF16),
            pltpu.VMEM((STEPS, HALVES, m, part, width), BF16),
            pltpu.VMEM((HALVES, part, width), F32),
            pltpu.VMEM((STEPS, HALVES, m, part, width), BF16),
            pltpu.VMEM((m, 8, rows), F32),
            pltpu.VMEM((m, 8, LANES), F32),
            pltpu.VMEM((n, 8, LANES), F32),
            dma((6,)),
            dma((3, m)),
            dma((3, m)),
            dma((STEPS, pairs, 2 * n)),
            dma((STEPS, pairs, 2, n)),
            dma((STEPS, (pairs + 2) * HALVES, m)),
            dma((STEPS, (pairs + 2) * HALVES, m)),
            dma((2, m)),
            dma((2, m)),
            dma((n,)),
            dma((n,)),
        ],
        compiler_params=pltpu.CompilerParams(
            collective_id=0, has_side_effects=True, vmem_limit_bytes=60 * 1024 * 1024
        ),
    )(
        latent,
        probe,
        time_embed.reshape(1, width),
        gain_attn.reshape(1, width),
        gain_mlp.reshape(1, width),
        w_query,
        w_key,
        w_value,
        w_out,
        w_in,
        w_down,
    )
    return (state, stats[0], stats[1], mean[0, 0])


def solution(mesh):
    return jax.shard_map(
        functools.partial(per_device, mesh.shape["seq"], mesh.shape["head"]),
        mesh=mesh,
        in_specs=(
            P("seq", None),
            P("seq", None),
            P(),
            P(),
            P(None, "head"),
            P(None, "head"),
            P(None, "head"),
            P("head", None),
            P(),
            P(None, "head"),
            P("head", None),
        ),
        out_specs=(P("seq", None), P("seq"), P("seq"), P()),
        check_vma=False,
    )
```

profile of v0, /device:TPU:0, one launch (start us, length us, event | category | flops | bytes accessed | tf_op | source)
XLA Modules:
  0.0 93.8 jit_solution(1907253678768312564)
XLA Ops:
  0.6 88.8 %shard_map.138 = (f32[128,1024]{1,0:T(8,128)}, f32[8,128]{1,0:T(8,128)}, f32[8,128]{1,0:T(8,128)}) custom-call(bf16[128,1024]{1,0:T(8,128)(2,1)} %latent.1, bf16[128,1024]{1,0:T(8,128)(2,1)} %probe.1, f32[1,1024]{1,0:T(1,128)} %bitcast.8, f32[1,1024]{1,0:T(1,128)} %bitcast.9, f32[1,1024]{1,0:T(1,128)} %bitcast.10, bf16[1024,256]{1,0:T(8,128)(2,1)} %w_query.1, ...), custom_call_target="tpu_custom_call" | custom-call | tf_op jit(solution)/shard_map/pallas_call | solution.py:500
  89.5 1.2 %slice.11 = f32[1,1]{1,0:T(1,128)} slice(f32[8,128]{1,0:T(8,128)} %get-tuple-element.9), slice={[0:1], [0:1]} | slice | bytes 8 | tf_op jit(solution)/shard_map/slice | solution.py:557
  90.6 1.3 %slice_bitcast_fusion = (f32[128]{0:T(128)}, f32[128]{0:T(128)}) fusion(f32[8,128]{1,0:T(8,128)} %get-tuple-element.8), kind=kLoop, calls=%fused_computation | loop fusion | bytes 2048 | tf_op jit(solution)/shard_map/squeeze | solution.py:557
  91.9 1.9 %copy.16 = f32[128,1024]{1,0:T(8,128)} copy(f32[128,1024]{1,0:T(8,128)} %get-tuple-element.16) | data formatting | bytes 1048576
where the time goes:
time: 94.1 us; the launch traced here: 93.8 us
  Pallas kernels  88.8 us (94%)
  local copies, waits for them, and re-layouts  4.34 us (5%)
    pallas_call x1, Pallas kernels, per_device(): pl.pallas_call(functools.partial(flow_kernel, n, m), out_shape=(jax.Shape...  88.8 us
    unnamed x1, local copies, waits for them, and re-layouts  1.88 us

commit v1 on v0

v1 whole, which is shorter than its diff:
```python
import functools
import math

import jax
import jax.numpy as jnp
from jax import lax
from jax.experimental import pallas as pl
from jax.experimental.pallas import tpu as pltpu
from jax.sharding import PartitionSpec as P

HEAD_DIM = 64
STEPS = 2
EPSILON = 1e-05
GELU_COEF = 0.044715
ROOT_TWO_PI = math.sqrt(2.0 / math.pi)
LANES = 128
CHUNKS = 2
BF16 = jnp.bfloat16
F32 = jnp.float32


def norm_scale(values):
    return lax.rsqrt(jnp.mean(values * values, axis=-1, keepdims=True) + EPSILON)


def norm_tangent(values, tangent, inverse, norm_gain):
    inner_mean = jnp.mean(values * tangent, axis=-1, keepdims=True)
    cubed = inverse * inverse * inverse
    return ((tangent * inverse - values * (cubed * inner_mean)) * norm_gain).astype(BF16)


def gelu_slope(pre_act):
    square = pre_act * pre_act
    tanh_value = jnp.tanh(ROOT_TWO_PI * pre_act * (1.0 + GELU_COEF * square))
    half = 0.5 * (1.0 + tanh_value)
    slope_value = half + 0.5 * pre_act * (1.0 - tanh_value * tanh_value) * (
        ROOT_TWO_PI * (1.0 + 3.0 * GELU_COEF * square)
    )
    return ((pre_act * half).astype(BF16), slope_value)


def dot(a, b):
    return jnp.dot(a, b, preferred_element_type=F32)


def dot_t(a, b):
    return lax.dot_general(a, b, (((1,), (1,)), ((), ())), preferred_element_type=F32)


def flow_kernel(
    n,
    m,
    latent,
    probe,
    time_embed,
    gain_attn,
    gain_mlp,
    w_query,
    w_key,
    w_value,
    w_out,
    w_in,
    w_down,
    latent_end,
    stats_out,
    mean_out,
    wqkv,
    wout,
    win,
    wdown,
    normed,
    qbuf,
    kbuf,
    vbuf,
    headall,
    inbuf,
    probe_down,
    weightbuf,
    primbuf,
    totalbuf,
    midbuf,
    slopebuf,
    partial,
    rssend,
    rsrecv,
    state,
    delta,
    tracebuf,
    sumbuf,
    lsem,
    wsend,
    wrecv,
    gsend,
    grecv,
    kvsend,
    kvrecv,
    zsend,
    zrecv,
    tsend,
    trecv,
    msend,
    mrecv,
):
    s = lax.axis_index("seq")
    z = lax.axis_index("head")
    rows, width = latent.shape
    part = rows // m
    piece = width // CHUNKS
    cols = w_query.shape[1]
    pairs = cols // LANES
    frames = rows * n
    near = n == 8

    def flip(bit):
        return s + bit - 2 * bit * lax.rem(s // bit, 2)

    def zpeer(d):
        return lax.rem(z + d, m)

    def zfrom(d):
        return lax.rem(z + m - d, m)

    def remote(src, dst, send, recv, target_s, target_z):
        return pltpu.make_async_remote_copy(
            src_ref=src,
            dst_ref=dst,
            send_sem=send,
            recv_sem=recv,
            device_id=(target_s, target_z),
            device_id_type=pl.DeviceIdType.MESH,
        )

    scope = [None]

    def S(name):
        if scope[0] is not None:
            scope[0].__exit__(None, None, None)
        scope[0] = None
        if name is not None:
            scope[0] = jax.named_scope(name)
            scope[0].__enter__()

    S("start")
    loads = [
        pltpu.make_async_copy(w_query, wqkv.at[:, pl.ds(0, cols)], lsem.at[0]),
        pltpu.make_async_copy(w_key, wqkv.at[:, pl.ds(cols, cols)], lsem.at[1]),
        pltpu.make_async_copy(w_value, wqkv.at[:, pl.ds(2 * cols, cols)], lsem.at[2]),
        pltpu.make_async_copy(w_out, wout.at[z], lsem.at[3]),
        pltpu.make_async_copy(w_in, win, lsem.at[4]),
        pltpu.make_async_copy(w_down, wdown, lsem.at[5]),
    ]
    for index in (3, 1, 2, 0, 5, 4):
        loads[index].start()

    barrier = pltpu.get_barrier_semaphore()

    def everyone():
        for a in range(n):
            for b in range(m):
                if a or b:
                    yield a * m + b, lax.rem(s + a, n), lax.rem(z + b, m)

    for _, target_s, target_z in everyone():
        pl.semaphore_signal(
            barrier, inc=1, device_id=(target_s, target_z), device_id_type=pl.DeviceIdType.MESH
        )

    own_rows = pl.ds(pl.multiple_of(z * part, part), part)
    direction = probe[...].astype(F32)

    def norm_inputs(values):
        inverse = norm_scale(values)
        normed[:rows, :] = (values * inverse * gain_attn[...]).astype(BF16)
        return inverse

    def norm_inputs_tangent(values, inverse):
        normed[rows:, :] = norm_tangent(
            values, probe[...].astype(F32), inverse, gain_attn[...]
        )

    first_values = latent[...].astype(F32)
    inbuf[...] = first_values
    inverse = norm_inputs(first_values)
    norm_inputs_tangent(first_values, inverse)
    state[...] = latent[own_rows, :].astype(F32)

    S("barrier")
    pl.semaphore_wait(barrier, n * m - 1)

    partner = flip(1)
    xn, yn = flip(2), flip(4)
    dn = yn + 2 - 4 * lax.rem(yn // 2, 2)

    def exchange(view, send_sem, recv_sem):
        sends = []

        def give(which, slot, target, at):
            copy = remote(
                view(which, slot),
                view(which, slot),
                send_sem(len(sends)),
                recv_sem(which, at),
                target,
                z,
            )
            copy.start()
            sends.append(copy)

        def got(which, slot, at):
            pltpu.make_async_copy(
                view(which, slot), view(which, slot), recv_sem(which, at)
            ).wait()

        def own(which):
            if near:
                first, second = ((xn, 2), (yn, 4)) if which == 0 else ((yn, 4), (xn, 2))
                give(which, s, *first)
                give(which, s, *second)
                give(which, s, partner, 1)
            else:
                for d in range(1, n):
                    give(which, s, lax.rem(s + d, n), d)

        def relay():
            if near:
                got(0, xn, 2)
                give(0, xn, yn, 6)
                got(1, yn, 4)
                give(1, yn, xn, 6)
                give(0, xn, partner, 3)
                give(1, yn, partner, 5)

        def rest():
            if near:
                got(0, yn, 4)
                give(0, yn, partner, 5)
                got(1, xn, 2)
                give(1, xn, partner, 3)
                got(0, dn, 6)
                give(0, dn, partner, 7)
                got(1, dn, 6)
                give(1, dn, partner, 7)

        def finish():
            if near:
                slots = ((s, 1), (xn, 3), (yn, 5), (dn, 7))
                for which in range(2):
                    for slot, at in slots:
                        got(which, slot + 1 - 2 * lax.rem(slot, 2), at)
            else:
                for which in range(2):
                    for d in range(1, n):
                        got(which, lax.rem(s + n - d, n), d)

        def drain():
            for copy in sends:
                copy.wait_send()

        return own, relay, rest, finish, drain

    def kv_exchange(k, t, p):
        bufs = (kbuf, vbuf)
        return exchange(
            lambda which, slot: bufs[which].at[k, t, p, slot],
            lambda index: kvsend.at[k, t, p, index],
            lambda which, at: kvrecv.at[k, t, p, which, at],
        )

    block = cols // n if near else cols
    strip = block // 2
    loads[3].wait()

    def block_at(slot):
        if near:
            return pl.ds(pl.multiple_of(slot * block, block), block)
        return pl.ds(0, cols)

    def strip_at(which, slot):
        return pl.ds(pl.multiple_of(slot * block + which * strip, strip), strip)

    fetch_order = [1, m - 1] + list(range(2, m - 1))
    fetches = {}
    for d in fetch_order:
        fetches[d] = remote(
            wout.at[z, block_at(s)],
            wout.at[z, block_at(s)],
            wsend.at[d],
            wrecv.at[d],
            s,
            zpeer(d),
        )
        fetches[d].start()

    def shard_exchange(d):
        return exchange(
            lambda which, slot: wout.at[zfrom(d), strip_at(which, slot)],
            lambda index: gsend.at[d, index],
            lambda which, at: grecv.at[d, which, at],
        )

    shards = {d: shard_exchange(d) for d in fetch_order} if near else {}

    def shard_own(d):
        fetches[d].wait_recv()
        if near:
            shards[d][0](0)
            shards[d][0](1)

    def z_start(k, phase, src_of, dst):
        copies = []
        for d in range(m - 1, 0, -1):
            copy = remote(
                src_of(zpeer(d)), dst, zsend.at[k, phase, d], zrecv.at[k, phase, d], s, zpeer(d)
            )
            copy.start()
            copies.append(copy)
        return copies

    def z_wait(copies):
        for copy in copies:
            copy.wait_send()
            copy.wait_recv()

    lane = lax.broadcasted_iota(jnp.int32, (1, LANES), 1)
    first = (lane // HEAD_DIM) == 0
    scale = HEAD_DIM ** (-0.5)

    def project(k, which, t):
        if k == 0 and t == 0:
            loads[which].wait()
        weight = wqkv[:, which * cols : (which + 1) * cols]
        return dot(normed[t * rows : (t + 1) * rows, :], weight).astype(BF16)

    def keep_pairs(ref, k, t, value):
        for p in range(pairs):
            ref[k, t, p, s] = value[:, p * LANES : (p + 1) * LANES]

    def two_heads(value):
        zero = jnp.zeros_like(value)
        return jnp.concatenate(
            [jnp.where(first, value, zero), jnp.where(first, zero, value)], axis=0
        )

    def join_heads(value):
        return jnp.where(first, value[:rows], value[rows:]).astype(BF16)

    def attention(k, p):
        keys = kbuf[k, 0, p].reshape(frames, LANES)
        vals = vbuf[k, 0, p].reshape(frames, LANES)
        scores = dot_t(two_heads(qbuf[0, p]), keys) * scale
        weights = jnp.exp(scores - jnp.max(scores, axis=-1, keepdims=True))
        total = jnp.sum(weights, axis=-1, keepdims=True)
        weightbuf[p] = weights
        prim = dot(weights.astype(BF16), vals) / total
        primbuf[p] = prim
        totalbuf[p] = jnp.broadcast_to(total, (2 * rows, LANES))
        headall[k, 0, p, z] = join_heads(prim)

    def attention_tangent(k, p):
        both_keys = jnp.concatenate(
            [kbuf[k, 0, p].reshape(frames, LANES), kbuf[k, 1, p].reshape(frames, LANES)], axis=1
        )
        vals = vbuf[k, 0, p].reshape(frames, LANES)
        val_tang = vbuf[k, 1, p].reshape(frames, LANES)
        both = jnp.concatenate([two_heads(qbuf[1, p]), two_heads(qbuf[0, p])], axis=1)
        score_tang = dot_t(both, both_keys) * scale
        weights = weightbuf[p]
        weighted = weights * score_tang
        carried = jnp.sum(weighted, axis=-1, keepdims=True)
        mixed = dot(weighted.astype(BF16), vals) + dot(weights.astype(BF16), val_tang)
        total = totalbuf[p]
        tang = mixed / total - (carried / total) * primbuf[p]
        headall[k, 1, p, z] = join_heads(tang)

    def heads_start(k, t, p):
        return z_start(k, t * pairs + p, lambda j: headall.at[k, t, p, z], headall.at[k, t, p, z])

    def out_project(k, t):
        heads = [headall[k, t, p, j] for j in range(m) for p in range(pairs)]
        return dot(jnp.concatenate(heads, axis=1), wout[...].reshape(m * cols, width))

    def mlp(k):
        attn = out_project(k, 0)
        mid = inbuf[...] + attn
        midbuf[...] = mid
        scaled = (mid * norm_scale(mid) * gain_mlp[...]).astype(BF16)
        if k == 0:
            loads[4].wait()
        act, slope = gelu_slope(dot(scaled, win[...]))
        slopebuf[...] = slope
        copies = []
        for c in range(CHUNKS):
            at = slice(c * piece, (c + 1) * piece)
            terms = dot(act, wdown[:, at])
            rssend[k, c] = terms.astype(BF16).reshape(m, part, piece)
            copies.append(
                z_start(
                    k,
                    2 * pairs + c,
                    lambda j: rssend.at[k, c, j],
                    rsrecv.at[k, c, z],
                )
            )
            partial[:, at] = attn[:, at] + terms
        return copies

    def mlp_tangent(k):
        attn_tang = out_project(k, 1)
        probing = probe[...].astype(F32)
        mid = midbuf[...]
        tangent = norm_tangent(mid, probing + attn_tang, norm_scale(mid), gain_mlp[...])
        act_tang = (slopebuf[...] * dot(tangent, win[...])).astype(BF16)
        return jnp.sum(probing * attn_tang, axis=-1, keepdims=True) / m + jnp.sum(
            act_tang.astype(F32) * probe_down[...], axis=-1, keepdims=True
        )

    trace = None
    tangent_heads = None
    all_exchanges = []

    for k in range(STEPS):
        last = k == STEPS - 1
        prims = [kv_exchange(k, 0, p) for p in range(pairs)]
        tangs = [kv_exchange(k, 1, p) for p in range(pairs)]
        all_exchanges += prims + tangs

        S(f"projk_{k}")
        keep_pairs(kbuf, k, 0, project(k, 1, 0))
        prims[0][0](0)
        S(f"projv_{k}")
        keep_pairs(vbuf, k, 0, project(k, 2, 0))
        prims[0][0](1)
        for p in range(1, pairs):
            prims[p][0](0)
            prims[p][0](1)
        if k > 0:
            S(f"tattn_{k-1}b")
            tangent_heads = [heads_start(k - 1, 1, p) for p in range(pairs)]
            norm_inputs_tangent(inbuf[...], inverse)
        S(f"projq_{k}")
        query = project(k, 0, 0)
        for p in range(pairs):
            qbuf[0, p] = query[:, p * LANES : (p + 1) * LANES]
        S(f"projt_{k}")
        keep_pairs(kbuf, k, 1, project(k, 1, 1))
        keep_pairs(vbuf, k, 1, project(k, 2, 1))
        S(f"relay0_{k}")
        prims[0][1]()
        S(f"projt2_{k}")
        query = project(k, 0, 1)
        for p in range(pairs):
            qbuf[1, p] = query[:, p * LANES : (p + 1) * LANES]
        S(f"relay1_{k}")
        for p in range(1, pairs):
            prims[p][1]()
        if k == 0:
            S(f"shard0_{k}")
            shard_own(fetch_order[0])
        else:
            for p in range(pairs):
                tangs[p][0](0)
                tangs[p][0](1)
        S(f"rest0_{k}")
        prims[0][2]()
        S(f"finish0_{k}")
        prims[0][3]()

        head_copies = []
        for p in range(pairs):
            if p > 0:
                S(f"rest1_{k}")
                prims[p][2]()
                prims[p][3]()
            S(f"attn_{k}_{p}")
            attention(k, p)
            head_copies.append(heads_start(k, 0, p))
            if k == 0 and p == 0:
                S(f"shard1_{k}")
                for d in fetch_order[1:]:
                    shard_own(d)

        if k == 0:
            S("probe_down")
            loads[5].wait()
            probe_down[...] = dot_t(probe[...], wdown[...])
            S("shard_relay")
            for d in shards:
                shards[d][1]()
            for p in range(pairs):
                tangs[p][0](0)
                tangs[p][0](1)
            S("shard_rest")
            for d in shards:
                shards[d][2]()
            for d in shards:
                shards[d][3]()
        else:
            for p in range(pairs):
                S(f"trelay_{k}_{p}")
                tangs[p][1]()
            for p in range(pairs):
                S(f"trest_{k}_{p}")
                tangs[p][2]()
                tangs[p][3]()
                S(f"tattn_{k}_{p}")
                attention_tangent(k, p)
                last_heads = heads_start(k, 1, p)
                later_heads = [last_heads] if p == 0 else later_heads + [last_heads]
            S(f"theads_{k-1}")
            for copies in tangent_heads:
                z_wait(copies)
            S(f"tmlp_{k-1}")
            trace = mlp_tangent(k - 1)
            tangent_heads = later_heads

        S(f"heads_{k}")
        for copies in head_copies:
            z_wait(copies)
        S(f"mlp_{k}")
        rs_copies = mlp(k)

        if not last:
            for p in range(pairs):
                S(f"trelay_{k}_{p}")
                tangs[p][1]()
            for p in range(pairs):
                S(f"trest_{k}_{p}")
                tangs[p][2]()
                tangs[p][3]()
                S(f"tattn_{k}_{p}")
                attention_tangent(k, p)
        else:
            S(f"theads_{k}")
            for copies in tangent_heads:
                z_wait(copies)
            S(f"tmlp_{k}")
            trace = trace + mlp_tangent(k)
            column = trace / (STEPS * width)
            trace_sum = jnp.sum(column, axis=0, keepdims=True)
            tracebuf[z] = jnp.transpose(jnp.broadcast_to(column, (rows, LANES)))[:8, :]
            trace_copies = []
            for d in range(1, m):
                copy = remote(
                    tracebuf.at[z], tracebuf.at[z], tsend.at[d], trecv.at[d], s, zpeer(d)
                )
                copy.start()
                trace_copies.append(copy)

        delta_copies = []
        squares = jnp.zeros((1, 1), F32)
        for c in range(CHUNKS):
            at = slice(c * piece, (c + 1) * piece)
            S(f"rswait_{k}_{c}")
            z_wait(rs_copies[c])
            S(f"field_{k}_{c}")
            field = partial[own_rows, at]
            for d in range(1, m):
                field = field + rsrecv[k, c, zfrom(d)].astype(F32)
            new_state = state[:, at] + field / STEPS
            state[:, at] = new_state
            delta[k, c, z] = (new_state - latent[own_rows, at].astype(F32)).astype(BF16)
            delta_copies.append(
                z_start(
                    k,
                    2 * pairs + CHUNKS + c,
                    lambda j: delta.at[k, c, z],
                    delta.at[k, c, z],
                )
            )
            if last:
                by_row = jnp.sum(new_state * new_state, axis=-1, keepdims=True)
                squares = squares + jnp.sum(by_row, axis=0, keepdims=True)
        if last:
            S("share")
            place = s * m + z
            sumbuf[place] = jnp.broadcast_to(trace_sum - 0.5 * squares / width, (1, LANES))
            mean_copies = []
            for index, target_s, target_z in everyone():
                copy = remote(
                    sumbuf.at[place],
                    sumbuf.at[place],
                    msend.at[index],
                    mrecv.at[index],
                    target_s,
                    target_z,
                )
                copy.start()
                mean_copies.append(copy)
            z_wait(trace_copies)
            trace_row = jnp.sum(tracebuf[...], axis=0)

        norm_sum = None
        for c in range(CHUNKS):
            at = slice(c * piece, (c + 1) * piece)
            S(f"deltawait_{k}_{c}")
            z_wait(delta_copies[c])
            S(f"norm_{k}_{c}")
            following = latent[:, at].astype(F32) + delta[k, c].reshape(rows, piece).astype(F32)
            if last:
                latent_end[:, at] = following
                norm_part = jnp.sum(following * following, axis=-1, keepdims=True)
                norm_sum = norm_part if norm_sum is None else norm_sum + norm_part
            else:
                inbuf[:, at] = following + ((k + 1) / STEPS) * time_embed[:, at]
        if not last:
            inverse = norm_inputs(inbuf[...])

    S("tail")
    norm_row = jnp.transpose(jnp.broadcast_to(norm_sum, (rows, LANES)))[:8]
    half_log = 0.5 * math.log(2.0 * math.pi)
    first_row = lax.broadcasted_iota(jnp.int32, (8, rows), 0) == 0
    stats_out[...] = jnp.where(
        first_row, trace_row, trace_row - 0.5 * norm_row / width - half_log
    )
    for exchanged in all_exchanges + [shards[d] for d in shards]:
        exchanged[4]()
    for d in fetches:
        fetches[d].wait_send()
    S("meanwait")
    z_wait(mean_copies)
    total = jnp.sum(sumbuf[...], axis=0)
    mean_out[...] = jnp.broadcast_to(total / frames - half_log, (8, LANES))
    S(None)


def per_device(
    n,
    m,
    latent,
    probe,
    time_embed,
    gain_attn,
    w_query,
    w_key,
    w_value,
    w_out,
    gain_mlp,
    w_in,
    w_down,
):
    rows, width = latent.shape
    cols = w_query.shape[1]
    hidden = w_in.shape[1]
    part = rows // m
    piece = width // CHUNKS
    pairs = cols // LANES
    frames = rows * n
    vmem = pl.BlockSpec(memory_space=pltpu.VMEM)
    anyspace = pl.BlockSpec(memory_space=pl.ANY)
    dma = pltpu.SemaphoreType.DMA
    phases = 2 * pairs + 2 * CHUNKS
    state, stats, mean = pl.pallas_call(
        functools.partial(flow_kernel, n, m),
        out_shape=(
            jax.ShapeDtypeStruct((rows, width), F32),
            jax.ShapeDtypeStruct((8, rows), F32),
            jax.ShapeDtypeStruct((8, LANES), F32),
        ),
        in_specs=[vmem] * 5 + [anyspace] * 6,
        out_specs=(vmem, vmem, vmem),
        scratch_shapes=[
            pltpu.VMEM((width, 3 * cols), BF16),
            pltpu.VMEM((m, cols, width), BF16),
            pltpu.VMEM((width, hidden), BF16),
            pltpu.VMEM((hidden, width), BF16),
            pltpu.VMEM((2 * rows, width), BF16),
            pltpu.VMEM((2, pairs, rows, LANES), BF16),
            pltpu.VMEM((STEPS, 2, pairs, n, rows, LANES), BF16),
            pltpu.VMEM((STEPS, 2, pairs, n, rows, LANES), BF16),
            pltpu.VMEM((STEPS, 2, pairs, m, rows, LANES), BF16),
            pltpu.VMEM((rows, width), F32),
            pltpu.VMEM((rows, hidden), F32),
            pltpu.VMEM((pairs, 2 * rows, frames), F32),
            pltpu.VMEM((pairs, 2 * rows, LANES), F32),
            pltpu.VMEM((pairs, 2 * rows, LANES), F32),
            pltpu.VMEM((rows, width), F32),
            pltpu.VMEM((rows, hidden), F32),
            pltpu.VMEM((rows, width), F32),
            pltpu.VMEM((STEPS, CHUNKS, m, part, piece), BF16),
            pltpu.VMEM((STEPS, CHUNKS, m, part, piece), BF16),
            pltpu.VMEM((part, width), F32),
            pltpu.VMEM((STEPS, CHUNKS, m, part, piece), BF16),
            pltpu.VMEM((m, 8, rows), F32),
            pltpu.VMEM((n * m, 1, LANES), F32),
            dma((6,)),
            dma((m,)),
            dma((m,)),
            dma((m, 2 * n)),
            dma((m, 2, n)),
            dma((STEPS, 2, pairs, 2 * n)),
            dma((STEPS, 2, pairs, 2, n)),
            dma((STEPS, phases, m)),
            dma((STEPS, phases, m)),
            dma((m,)),
            dma((m,)),
            dma((n * m,)),
            dma((n * m,)),
        ],
        compiler_params=pltpu.CompilerParams(
            collective_id=0, has_side_effects=True, vmem_limit_bytes=60 * 1024 * 1024
        ),
    )(
        latent,
        probe,
        time_embed.reshape(1, width),
        gain_attn.reshape(1, width),
        gain_mlp.reshape(1, width),
        w_query,
        w_key,
        w_value,
        w_out,
        w_in,
        w_down,
    )
    return (state, stats[0], stats[1], mean[0, 0])


def solution(mesh):
    return jax.shard_map(
        functools.partial(per_device, mesh.shape["seq"], mesh.shape["head"]),
        mesh=mesh,
        in_specs=(
            P("seq", None),
            P("seq", None),
            P(),
            P(),
            P(None, "head"),
            P(None, "head"),
            P(None, "head"),
            P("head", None),
            P(),
            P(None, "head"),
            P("head", None),
        ),
        out_specs=(P("seq", None), P("seq"), P("seq"), P()),
        check_vma=False,
    )
```

time: 94.1 us -> 87.6 us (0.931)
  Pallas kernels: 88.8 us -> 82.3 us
    pallas_call x1, Pallas kernels: 88.8 us -> 82.3 us  [per_device(): pl.pallas_call(functools.partial(flow_kernel, n, m), out_shape=(jax.Shape...]
where the time goes in v1:
time: 87.6 us; the launch traced here: 87.3 us
  Pallas kernels  82.3 us (94%)
  local copies, waits for them, and re-layouts  4.34 us (5%)
    pallas_call x1, Pallas kernels, per_device(): pl.pallas_call(functools.partial(flow_kernel, n, m), out_shape=(jax.Shape...  82.3 us
    unnamed x1, local copies, waits for them, and re-layouts  1.88 us

profile of v1, /device:TPU:0, one launch (start us, length us, event | category | flops | bytes accessed | tf_op | source)
XLA Modules:
  0.0 87.3 jit_solution(14881699996830351723)
XLA Ops:
  0.6 82.3 %shard_map.138 = (f32[128,1024]{1,0:T(8,128)}, f32[8,128]{1,0:T(8,128)}, f32[8,128]{1,0:T(8,128)}) custom-call(bf16[128,1024]{1,0:T(8,128)(2,1)} %latent.1, bf16[128,1024]{1,0:T(8,128)(2,1)} %probe.1, f32[1,1024]{1,0:T(1,128)} %bitcast.8, f32[1,1024]{1,0:T(1,128)} %bitcast.9, f32[1,1024]{1,0:T(1,128)} %bitcast.10, bf16[1024,256]{1,0:T(8,128)(2,1)} %w_query.1, ...), custom_call_target="tpu_custom_call" | custom-call | tf_op jit(solution)/shard_map/pallas_call | solution.py:652
  83.0 1.2 %slice.11 = f32[1,1]{1,0:T(1,128)} slice(f32[8,128]{1,0:T(8,128)} %get-tuple-element.9), slice={[0:1], [0:1]} | slice | bytes 8 | tf_op jit(solution)/shard_map/slice | solution.py:715
  84.1 1.3 %slice_bitcast_fusion = (f32[128]{0:T(128)}, f32[128]{0:T(128)}) fusion(f32[8,128]{1,0:T(8,128)} %get-tuple-element.8), kind=kLoop, calls=%fused_computation | loop fusion | bytes 2048 | tf_op jit(solution)/shard_map/squeeze | solution.py:715
  85.4 1.9 %copy.16 = f32[128,1024]{1,0:T(8,128)} copy(f32[128,1024]{1,0:T(8,128)} %get-tuple-element.16) | data formatting | bytes 1048576

commit v2 on v1

v2 whole, which is shorter than its diff:
```python
import functools
import math

import jax
import jax.numpy as jnp
from jax import lax
from jax.experimental import pallas as pl
from jax.experimental.pallas import tpu as pltpu
from jax.sharding import PartitionSpec as P

HEAD_DIM = 64
STEPS = 2
EPSILON = 1e-05
GELU_COEF = 0.044715
ROOT_TWO_PI = math.sqrt(2.0 / math.pi)
LANES = 128
CHUNKS = 2
BF16 = jnp.bfloat16
F32 = jnp.float32


def norm_scale(values):
    return lax.rsqrt(jnp.mean(values * values, axis=-1, keepdims=True) + EPSILON)


def norm_tangent(values, tangent, inverse, norm_gain):
    inner_mean = jnp.mean(values * tangent, axis=-1, keepdims=True)
    cubed = inverse * inverse * inverse
    return ((tangent * inverse - values * (cubed * inner_mean)) * norm_gain).astype(BF16)


def gelu_slope(pre_act):
    square = pre_act * pre_act
    tanh_value = jnp.tanh(ROOT_TWO_PI * pre_act * (1.0 + GELU_COEF * square))
    half = 0.5 * (1.0 + tanh_value)
    slope_value = half + 0.5 * pre_act * (1.0 - tanh_value * tanh_value) * (
        ROOT_TWO_PI * (1.0 + 3.0 * GELU_COEF * square)
    )
    return ((pre_act * half).astype(BF16), slope_value)


def dot(a, b):
    return jnp.dot(a, b, preferred_element_type=F32)


def dot_t(a, b):
    return lax.dot_general(a, b, (((1,), (1,)), ((), ())), preferred_element_type=F32)


def flow_kernel(
    n,
    m,
    latent,
    probe,
    time_embed,
    gain_attn,
    gain_mlp,
    w_query,
    w_key,
    w_value,
    w_out,
    w_in,
    w_down,
    latent_end,
    stats_out,
    mean_out,
    wqkv,
    wout,
    win,
    wdown,
    normed,
    qbuf,
    kvbuf,
    headall,
    inbuf,
    probe_down,
    weightbuf,
    primbuf,
    totalbuf,
    midbuf,
    slopebuf,
    partial,
    rssend,
    passbuf,
    rsrecv,
    state,
    delta,
    tracebuf,
    sumbuf,
    lsem,
    fetchsem,
    shardsem,
    kvsend,
    primrecv,
    tangrecv,
    zsem,
    allsem,
):
    s = lax.axis_index("seq")
    z = lax.axis_index("head")
    rows, width = latent.shape
    part = rows // m
    piece = width // CHUNKS
    cols = w_query.shape[1]
    pairs = cols // LANES
    frames = rows * n
    near = n == 8

    def flip(bit):
        return s + bit - 2 * bit * lax.rem(s // bit, 2)

    def zflip(mask):
        twos = z // 2
        ones = z - 2 * twos
        if mask & 1:
            ones = 1 - ones
        if mask & 2:
            twos = 1 - twos
        return 2 * twos + ones

    def zpeer(d):
        return lax.rem(z + d, m)

    def zfrom(d):
        return lax.rem(z + m - d, m)

    def remote(src, dst, send, recv, target_s, target_z):
        return pltpu.make_async_remote_copy(
            src_ref=src,
            dst_ref=dst,
            send_sem=send,
            recv_sem=recv,
            device_id=(target_s, target_z),
            device_id_type=pl.DeviceIdType.MESH,
        )

    scope = [None]

    def S(name):
        if scope[0] is not None:
            scope[0].__exit__(None, None, None)
        scope[0] = None
        if name is not None:
            scope[0] = jax.named_scope(name)
            scope[0].__enter__()

    S("start")
    loads = [
        pltpu.make_async_copy(w_query, wqkv.at[:, pl.ds(0, cols)], lsem.at[0]),
        pltpu.make_async_copy(w_key, wqkv.at[:, pl.ds(cols, cols)], lsem.at[1]),
        pltpu.make_async_copy(w_value, wqkv.at[:, pl.ds(2 * cols, cols)], lsem.at[2]),
        pltpu.make_async_copy(w_out, wout.at[z], lsem.at[3]),
        pltpu.make_async_copy(w_in, win, lsem.at[4]),
        pltpu.make_async_copy(w_down, wdown, lsem.at[5]),
    ]
    for index in (3, 1, 2, 0, 5, 4):
        loads[index].start()

    barrier = pltpu.get_barrier_semaphore()

    peers = [(s, zpeer(d)) for d in range(1, m)] + [(lax.rem(s + d, n), z) for d in range(1, n)]
    for peer in peers:
        pl.semaphore_signal(barrier, inc=1, device_id=peer, device_id_type=pl.DeviceIdType.MESH)

    own_rows = pl.ds(pl.multiple_of(z * part, part), part)
    direction = probe[...].astype(F32)

    def norm_inputs(values):
        inverse = norm_scale(values)
        normed[:rows, :] = (values * inverse * gain_attn[...]).astype(BF16)
        return inverse

    def norm_inputs_tangent(values, inverse):
        normed[rows:, :] = norm_tangent(
            values, probe[...].astype(F32), inverse, gain_attn[...]
        )

    first_values = latent[...].astype(F32)
    inbuf[...] = first_values
    inverse = norm_inputs(first_values)
    norm_inputs_tangent(first_values, inverse)
    state[...] = latent[own_rows, :].astype(F32)

    S("barrier")
    pl.semaphore_wait(barrier, n + m - 2)

    partner = flip(1)
    xn, yn = flip(2), flip(4)
    dn = yn + 2 - 4 * lax.rem(yn // 2, 2)

    def exchange(view, landing, span, sends, lands, fine):
        count = [0]

        def give(which, slot, target, there, sem):
            remote(
                view(which, slot), landing(which, slot, there), sends, lands(sem), target, z
            ).start()
            count[0] += 1

        def got(sem, number):
            pltpu.make_async_copy(span(number), span(number), lands(sem)).wait()

        sems = (0, 1, 2, 3, 4, 5, 6) if fine else (0, 0, 1, 1, 1, 1, 2)

        def own(which):
            if near:
                over_x = (xn, 2, sems[0 if which == 0 else 3])
                over_y = (yn, 4, sems[2 if which == 0 else 1])
                for hop in (over_x, over_y) if which == 0 else (over_y, over_x):
                    give(which, 0, *hop)
                give(which, 0, partner, 1, sems[6])
            else:
                for d in range(1, n):
                    give(which, 0, lax.rem(s + d, n), n - d, sems[6])

        def relay():
            if near:
                got(sems[0], 1 if fine else 2)
                give(0, 2, yn, 6, sems[4])
                if fine:
                    got(sems[1], 1)
                give(1, 4, xn, 6, sems[5])
                give(0, 2, partner, 3, sems[6])
                give(1, 4, partner, 5, sems[6])

        def rest():
            if near:
                if not fine:
                    got(sems[2], 4)
                for which, slot, sem in ((0, 4, 2), (1, 2, 3), (0, 6, 4), (1, 6, 5)):
                    if fine:
                        got(sems[sem], 1)
                    give(which, slot, partner, slot + 1, sems[6])

        def finish():
            got(sems[6], n if near else 2 * n - 2)

        def drain():
            pltpu.make_async_copy(span(count[0]), span(count[0]), sends).wait()

        return own, relay, rest, finish, drain

    def kv_exchange(k, t, p):
        return exchange(
            lambda which, slot: kvbuf.at[k, t, p, which * n + slot],
            lambda which, slot, there: kvbuf.at[k, t, p, which * n + there],
            lambda number: kvbuf.at[k, t, p, pl.ds(0, number)],
            kvsend.at[k, t, p],
            lambda sem: tangrecv.at[k, p, sem] if t else primrecv.at[k, p, sem],
            t == 0,
        )

    line = m == 4
    inner = jnp.logical_and(z > 0, z < m - 1)
    sources = (1, 2, 3) if line else tuple(range(1, m))

    def zsource(index):
        return zflip(index) if line else zfrom(index)

    def waited(ref, sem):
        pltpu.make_async_copy(ref, ref, sem).wait()

    def z_gather(view, span, sem, own_sems=False):
        def landing(index):
            if own_sems:
                return sem(index)
            return sem(1) if line and index == 2 else sem(2)

        def send(block, target, index):
            remote(view(block), view(block), sem(0), landing(index), s, target).start()

        def start():
            if line:
                send(z, zflip(2), 2)
                send(z, zflip(1), 1)

                @pl.when(inner)
                def _():
                    send(z, zflip(3), 3)
            else:
                for d in range(m - 1, 0, -1):
                    send(z, zpeer(d), d)

        def relay():
            if line:
                waited(span(1), landing(2))

                @pl.when(inner)
                def _():
                    send(zflip(2), zflip(1), 3)

        def finish(index):
            if not (line and index == 2):
                waited(span(1), landing(index))

        def finish_all():
            waited(span(2 if line else m - 1), sem(2))

        def drain():
            if line:

                @pl.when(inner)
                def _():
                    waited(span(4), sem(0))

                @pl.when(jnp.logical_not(inner))
                def _():
                    waited(span(2), sem(0))
            else:
                waited(span(m - 1), sem(0))

        return start, relay, finish, finish_all, drain

    def z_reduce(block, passed, landed, span, sem):
        def send(source, target, slot):
            landing = sem(1) if line and slot == 0 else sem(2)
            remote(source, landed(slot), sem(0), landing, s, target).start()

        def start():
            if line:

                @pl.when(jnp.logical_not(inner))
                def _():
                    send(block(zflip(3)), zflip(1), 0)
                    send(block(zflip(2)), zflip(2), 2)

                @pl.when(inner)
                def _():
                    send(block(zflip(3)), zflip(3), 3)

                send(block(zflip(1)), zflip(1), 1)
            else:
                for d in range(m - 1, 0, -1):
                    send(block(zpeer(d)), zpeer(d), d)

        def relay():
            if line:

                @pl.when(inner)
                def _():
                    waited(span(1), sem(1))
                    both = landed(0)[...].astype(F32) + block(zflip(2))[...].astype(F32)
                    passed[...] = both.astype(BF16)
                    send(passed, zflip(2), 2)

        def finish():
            if line:

                @pl.when(inner)
                def _():
                    waited(span(3), sem(2))

                @pl.when(jnp.logical_not(inner))
                def _():
                    waited(span(2), sem(2))
                    landed(3)[...] = jnp.zeros(landed(3).shape, BF16)
            else:
                waited(span(m - 1), sem(2))

        def drain():
            waited(span(3 if line else m - 1), sem(0))

        return start, relay, finish, drain

    block = cols // n if near else cols
    strip = block // 2
    loads[3].wait()

    def block_at(slot):
        if near:
            return pl.ds(pl.multiple_of(slot * block, block), block)
        return pl.ds(0, cols)

    def strip_at(which, slot):
        return pl.ds(pl.multiple_of(slot * block + which * strip, strip), strip)

    fetch = z_gather(
        lambda j: wout.at[j, block_at(s)],
        lambda number: wout.at[pl.ds(0, number), block_at(0)],
        lambda d: fetchsem.at[d],
        own_sems=True,
    )
    fetch[0]()

    def place(slot):
        where = (s, xn, yn, dn)[slot // 2]
        return where if slot % 2 == 0 else where + 1 - 2 * lax.rem(where, 2)

    def shard_exchange(d):
        return exchange(
            lambda which, slot: wout.at[zsource(d), strip_at(which, place(slot))],
            lambda which, slot, there: wout.at[zsource(d), strip_at(which, place(slot))],
            lambda number: wout.at[0, pl.ds(0, number * strip)],
            shardsem.at[d, 3],
            lambda sem: shardsem.at[d, sem],
            False,
        )

    shards = {d: shard_exchange(d) for d in sources} if near else {}

    def shard_own(d):
        fetch[2](d)
        if near:
            shards[d][0](0)
            shards[d][0](1)

    def shard_do(stage, chosen):
        if near:
            for d in chosen:
                shards[d][stage]()

    gathers = []

    def gather(k, phase, view, span):
        gathers.append(z_gather(view, span, lambda index: zsem.at[k, phase, index]))
        return gathers[-1]

    def spread(ref, pair, targets, at):
        for target_s, target_z in targets:
            remote(
                ref.at[at], ref.at[at], allsem.at[pair], allsem.at[pair + 1], target_s, target_z
            ).start()

    def settle(ref, pair, targets):
        block = ref.at[pl.ds(0, len(targets))]
        waited(block, allsem.at[pair])
        waited(block, allsem.at[pair + 1])

    lane = lax.broadcasted_iota(jnp.int32, (1, LANES), 1)
    first = (lane // HEAD_DIM) == 0
    scale = HEAD_DIM ** (-0.5)

    def project(k, which, t):
        if k == 0 and t == 0:
            loads[which].wait()
        weight = wqkv[:, which * cols : (which + 1) * cols]
        return dot(normed[t * rows : (t + 1) * rows, :], weight).astype(BF16)

    def keep_pairs(which, k, t, value):
        for p in range(pairs):
            kvbuf[k, t, p, which * n] = value[:, p * LANES : (p + 1) * LANES]

    def whole(k, t, p, which):
        return kvbuf[k, t, p, which * n : (which + 1) * n].reshape(frames, LANES)

    def two_heads(value):
        zero = jnp.zeros_like(value)
        return jnp.concatenate(
            [jnp.where(first, value, zero), jnp.where(first, zero, value)], axis=0
        )

    def join_heads(value):
        return jnp.where(first, value[:rows], value[rows:]).astype(BF16)

    def attention(k, p):
        keys = whole(k, 0, p, 0)
        vals = whole(k, 0, p, 1)
        scores = dot_t(two_heads(qbuf[k, 0, p]), keys) * scale
        weights = jnp.exp(scores - jnp.max(scores, axis=-1, keepdims=True))
        total = jnp.sum(weights, axis=-1, keepdims=True)
        weightbuf[p] = weights
        prim = dot(weights.astype(BF16), vals) / total
        primbuf[p] = prim
        totalbuf[p] = jnp.broadcast_to(total, (2 * rows, LANES))
        headall[k, 0, p, z] = join_heads(prim)

    def attention_tangent(k, p):
        both_keys = jnp.concatenate([whole(k, 0, p, 0), whole(k, 1, p, 0)], axis=1)
        vals = whole(k, 0, p, 1)
        val_tang = whole(k, 1, p, 1)
        both = jnp.concatenate([two_heads(qbuf[k, 1, p]), two_heads(qbuf[k, 0, p])], axis=1)
        score_tang = dot_t(both, both_keys) * scale
        weights = weightbuf[p]
        weighted = weights * score_tang
        carried = jnp.sum(weighted, axis=-1, keepdims=True)
        mixed = dot(weighted.astype(BF16), vals) + dot(weights.astype(BF16), val_tang)
        total = totalbuf[p]
        tang = mixed / total - (carried / total) * primbuf[p]
        headall[k, 1, p, z] = join_heads(tang)

    def heads_gather(k, t, p):
        return gather(
            k,
            t * pairs + p,
            lambda j: headall.at[k, t, p, j],
            lambda number: headall.at[k, t, p, pl.ds(0, number)],
        )

    def out_project(k, t):
        heads = [headall[k, t, p, j] for j in range(m) for p in range(pairs)]
        return dot(jnp.concatenate(heads, axis=1), wout[...].reshape(m * cols, width))

    def mlp(k):
        attn = out_project(k, 0)
        mid = inbuf[...] + attn
        midbuf[...] = mid
        scaled = (mid * norm_scale(mid) * gain_mlp[...]).astype(BF16)
        if k == 0:
            loads[4].wait()
        act, slope = gelu_slope(dot(scaled, win[...]))
        slopebuf[...] = slope
        for c in range(CHUNKS):
            at = slice(c * piece, (c + 1) * piece)
            terms = dot(act, wdown[:, at])
            rssend[k, c] = terms.astype(BF16).reshape(m, part, piece)
            reduces[k][c][0]()
            partial[:, at] = attn[:, at] + terms

    def mlp_tangent(k):
        attn_tang = out_project(k, 1)
        probing = probe[...].astype(F32)
        mid = midbuf[...]
        tangent = norm_tangent(mid, probing + attn_tang, norm_scale(mid), gain_mlp[...])
        act_tang = (slopebuf[...] * dot(tangent, win[...])).astype(BF16)
        return jnp.sum(probing * attn_tang, axis=-1, keepdims=True) / m + jnp.sum(
            act_tang.astype(F32) * probe_down[...], axis=-1, keepdims=True
        )

    def reduce(k, c):
        phase = 2 * pairs + CHUNKS + c
        return z_reduce(
            lambda j: rssend.at[k, c, j],
            passbuf.at[k, c],
            lambda d: rsrecv.at[k, c, d],
            lambda number: rsrecv.at[k, c, pl.ds(0, number)],
            lambda index: zsem.at[k, phase, index],
        )

    reduces = [[reduce(k, c) for c in range(CHUNKS)] for k in range(STEPS)]
    prims = [[kv_exchange(k, 0, p) for p in range(pairs)] for k in range(STEPS)]
    tangs = [[kv_exchange(k, 1, p) for p in range(pairs)] for k in range(STEPS)]
    heads = [[heads_gather(k, 0, p) for p in range(pairs)] for k in range(STEPS)]
    tangent_heads = [[heads_gather(k, 1, p) for p in range(pairs)] for k in range(STEPS)]

    def delta_gather(k, c):
        return gather(
            k,
            2 * pairs + c,
            lambda j: delta.at[k, c, j],
            lambda number: delta.at[k, c, pl.ds(0, number)],
        )

    deltas = [[delta_gather(k, c) for c in range(CHUNKS)] for k in range(STEPS)]
    trace = None

    for k in range(STEPS):
        last = k == STEPS - 1

        S(f"projk_{k}")
        keep_pairs(0, k, 0, project(k, 1, 0))
        prims[k][0][0](0)
        S(f"projv_{k}")
        keep_pairs(1, k, 0, project(k, 2, 0))
        prims[k][0][0](1)
        for p in range(1, pairs):
            prims[k][p][0](0)
            prims[k][p][0](1)
        if k > 0:
            S(f"normt_{k}")
            for p in range(pairs):
                tangent_heads[k - 1][p][0]()
            norm_inputs_tangent(inbuf[...], inverse)
        S(f"projq_{k}")
        query = project(k, 0, 0)
        for p in range(pairs):
            qbuf[k, 0, p] = query[:, p * LANES : (p + 1) * LANES]
        S(f"projt_{k}")
        keep_pairs(0, k, 1, project(k, 1, 1))
        keep_pairs(1, k, 1, project(k, 2, 1))
        query = project(k, 0, 1)
        for p in range(pairs):
            qbuf[k, 1, p] = query[:, p * LANES : (p + 1) * LANES]
        S(f"relay0_{k}")
        prims[k][0][1]()
        if k == 0:
            S(f"fetchrelay_{k}")
            fetch[1]()
            shard_own(sources[0])
        S(f"relay1_{k}")
        for p in range(1, pairs):
            prims[k][p][1]()
        if k == 0:
            S(f"shard0_{k}")
            shard_own(sources[1])
        else:
            for p in range(pairs):
                tangs[k][p][0](0)
                tangs[k][p][0](1)
        S(f"rest0_{k}")
        prims[k][0][2]()
        if k > 0:
            S(f"trelayz_{k-1}")
            for p in range(pairs):
                tangent_heads[k - 1][p][1]()
        S(f"finish0_{k}")
        prims[k][0][3]()
        S(f"attn_{k}_0")
        attention(k, 0)
        heads[k][0][0]()
        if k == 0:
            S(f"shard1_{k}")
            shard_own(sources[2])
            shard_do(1, sources[:2])
        else:
            S(f"trelay_{k}_0")
            tangs[k][0][1]()
        for p in range(1, pairs):
            S(f"rest1_{k}")
            prims[k][p][2]()
            prims[k][p][3]()
            S(f"attn_{k}_{p}")
            attention(k, p)
            heads[k][p][0]()

        if k == 0:
            S("shard_rest")
            shard_do(2, sources[:2])
            shard_do(1, sources[2:])
            for p in range(pairs):
                tangs[k][p][0](0)
                tangs[k][p][0](1)
            S("probe_down")
            loads[5].wait()
            probe_down[...] = dot_t(probe[...], wdown[...])
            S("headrelay_0")
            for p in range(pairs):
                heads[k][p][1]()
            S("shard_finish")
            shard_do(3, sources[:2])
            shard_do(2, sources[2:])
            S("shard_finish2")
            shard_do(3, sources[2:])
        else:
            S(f"trelay_{k}_1")
            for p in range(1, pairs):
                tangs[k][p][1]()
            S(f"trest_{k}_0")
            tangs[k][0][2]()
            S(f"theads_{k-1}")
            for p in range(pairs):
                tangent_heads[k - 1][p][3]()
            S(f"tmlp_{k-1}")
            grown = mlp_tangent(k - 1)
            trace = grown if trace is None else trace + grown
            S(f"headrelay_{k}_0")
            heads[k][0][1]()
            S(f"tfinish_{k}_0")
            tangs[k][0][3]()
            S(f"tattn_{k}_0")
            attention_tangent(k, 0)
            tangent_heads[k][0][0]()
            for p in range(1, pairs):
                S(f"headrelay_{k}_{p}")
                heads[k][p][1]()
                S(f"tfinish_{k}_{p}")
                tangs[k][p][2]()
                tangs[k][p][3]()
                S(f"tattn_{k}_{p}")
                attention_tangent(k, p)
                if last:
                    tangent_heads[k][p][0]()

        S(f"heads_{k}")
        for p in range(pairs):
            heads[k][p][3]()
        S(f"mlp_{k}")
        mlp(k)

        if k == 0:
            for p in range(pairs):
                S(f"trelay_{k}_{p}")
                tangs[k][p][1]()
        for c in range(CHUNKS):
            S(f"rsrelay_{k}_{c}")
            reduces[k][c][1]()
        if last:
            S(f"threlay_{k}")
            for p in range(pairs):
                tangent_heads[k][p][1]()
            S(f"theads_{k}")
            for p in range(pairs):
                tangent_heads[k][p][3]()
            S(f"tmlp_{k}")
            trace = trace + mlp_tangent(k)
            column = trace / (STEPS * width)
            trace_sum = jnp.sum(column, axis=0, keepdims=True)
            tracebuf[z] = jnp.transpose(jnp.broadcast_to(column, (rows, LANES)))[:8, :]
            ring = [(s, zpeer(d)) for d in range(1, m)]
            spread(tracebuf, 0, ring, z)

        squares = jnp.zeros((1, 1), F32)
        for c in range(CHUNKS):
            at = slice(c * piece, (c + 1) * piece)
            S(f"rswait_{k}_{c}")
            reduces[k][c][2]()
            S(f"field_{k}_{c}")
            field = partial[own_rows, at]
            for d in sources:
                field = field + rsrecv[k, c, d].astype(F32)
            new_state = state[:, at] + field / STEPS
            state[:, at] = new_state
            delta[k, c, z] = (new_state - latent[own_rows, at].astype(F32)).astype(BF16)
            if last:
                by_row = jnp.sum(new_state * new_state, axis=-1, keepdims=True)
                squares = squares + jnp.sum(by_row, axis=0, keepdims=True)
                if c == CHUNKS - 1:
                    sumbuf[s * m + z] = jnp.broadcast_to(
                        trace_sum - 0.5 * squares / width, (1, LANES)
                    )
                    others = [
                        (lax.rem(s + a, n), lax.rem(z + b, m))
                        for a in range(n)
                        for b in range(m)
                        if a or b
                    ]
                    spread(sumbuf, 2, others, s * m + z)
            deltas[k][c][0]()
        if not last:
            for p in range(pairs):
                S(f"trest_{k}_{p}")
                tangs[k][p][2]()
            S(f"deltarelay_{k}")
            for c in range(CHUNKS):
                deltas[k][c][1]()
            for p in range(pairs):
                S(f"tfinish_{k}_{p}")
                tangs[k][p][3]()
                S(f"tattn_{k}_{p}")
                attention_tangent(k, p)
        else:
            S("deltarelay_1_0")
            deltas[k][0][1]()
            S("deltarelay_1_1")
            for c in range(1, CHUNKS):
                deltas[k][c][1]()
            settle(tracebuf, 0, ring)
            trace_row = jnp.sum(tracebuf[...], axis=0)

        norm_sum = None
        for c in range(CHUNKS):
            at = slice(c * piece, (c + 1) * piece)
            S(f"deltawait_{k}_{c}")
            deltas[k][c][3]()
            S(f"norm_{k}_{c}")
            following = latent[:, at].astype(F32) + delta[k, c].reshape(rows, piece).astype(F32)
            if last:
                latent_end[:, at] = following
                norm_part = jnp.sum(following * following, axis=-1, keepdims=True)
                norm_sum = norm_part if norm_sum is None else norm_sum + norm_part
            else:
                inbuf[:, at] = following + ((k + 1) / STEPS) * time_embed[:, at]
        if not last:
            inverse = norm_inputs(inbuf[...])

    S("tail")
    norm_row = jnp.transpose(jnp.broadcast_to(norm_sum, (rows, LANES)))[:8]
    half_log = 0.5 * math.log(2.0 * math.pi)
    first_row = lax.broadcasted_iota(jnp.int32, (8, rows), 0) == 0
    stats_out[...] = jnp.where(
        first_row, trace_row, trace_row - 0.5 * norm_row / width - half_log
    )
    for k in range(STEPS):
        for exchanged in prims[k] + tangs[k]:
            exchanged[4]()
        for reduced in reduces[k]:
            reduced[3]()
    for d in shards:
        shards[d][4]()
    for gathered in gathers + [fetch]:
        gathered[4]()
    S("meanwait")
    settle(sumbuf, 2, others)
    total = jnp.sum(sumbuf[...], axis=0)
    mean_out[...] = jnp.broadcast_to(total / frames - half_log, (8, LANES))
    S(None)


def finish_kernel(state, stats, mean, latent_end, trace, logp, total):
    latent_end[...] = state[...]
    trace[...] = stats[0:1, :]
    logp[...] = stats[1:2, :]
    total[...] = mean[0:1, 0:1]


def per_device(
    n,
    m,
    latent,
    probe,
    time_embed,
    gain_attn,
    w_query,
    w_key,
    w_value,
    w_out,
    gain_mlp,
    w_in,
    w_down,
):
    rows, width = latent.shape
    cols = w_query.shape[1]
    hidden = w_in.shape[1]
    part = rows // m
    piece = width // CHUNKS
    pairs = cols // LANES
    frames = rows * n
    vmem = pl.BlockSpec(memory_space=pltpu.VMEM)
    anyspace = pl.BlockSpec(memory_space=pl.ANY)
    dma = pltpu.SemaphoreType.DMA
    phases = 2 * pairs + 2 * CHUNKS
    state, stats, mean = pl.pallas_call(
        functools.partial(flow_kernel, n, m),
        out_shape=(
            jax.ShapeDtypeStruct((rows, width), F32),
            jax.ShapeDtypeStruct((8, rows), F32),
            jax.ShapeDtypeStruct((8, LANES), F32),
        ),
        in_specs=[vmem] * 5 + [anyspace] * 6,
        out_specs=(vmem, vmem, vmem),
        scratch_shapes=[
            pltpu.VMEM((width, 3 * cols), BF16),
            pltpu.VMEM((m, cols, width), BF16),
            pltpu.VMEM((width, hidden), BF16),
            pltpu.VMEM((hidden, width), BF16),
            pltpu.VMEM((2 * rows, width), BF16),
            pltpu.VMEM((STEPS, 2, pairs, rows, LANES), BF16),
            pltpu.VMEM((STEPS, 2, pairs, 2 * n, rows, LANES), BF16),
            pltpu.VMEM((STEPS, 2, pairs, m, rows, LANES), BF16),
            pltpu.VMEM((rows, width), F32),
            pltpu.VMEM((rows, hidden), F32),
            pltpu.VMEM((pairs, 2 * rows, frames), F32),
            pltpu.VMEM((pairs, 2 * rows, LANES), F32),
            pltpu.VMEM((pairs, 2 * rows, LANES), F32),
            pltpu.VMEM((rows, width), F32),
            pltpu.VMEM((rows, hidden), F32),
            pltpu.VMEM((rows, width), F32),
            pltpu.VMEM((STEPS, CHUNKS, m, part, piece), BF16),
            pltpu.VMEM((STEPS, CHUNKS, part, piece), BF16),
            pltpu.VMEM((STEPS, CHUNKS, m, part, piece), BF16),
            pltpu.VMEM((part, width), F32),
            pltpu.VMEM((STEPS, CHUNKS, m, part, piece), BF16),
            pltpu.VMEM((m, 8, rows), F32),
            pltpu.VMEM((n * m, 1, LANES), F32),
            dma((6,)),
            dma((m,)),
            dma((m, 4)),
            dma((STEPS, 2, pairs)),
            dma((STEPS, pairs, 7)),
            dma((STEPS, pairs, 3)),
            dma((STEPS, phases, 3)),
            dma((4,)),
        ],
        compiler_params=pltpu.CompilerParams(
            collective_id=0,
            has_side_effects=True,
            vmem_limit_bytes=60 * 1024 * 1024,
        ),
    )(
        latent,
        probe,
        time_embed.reshape(1, width),
        gain_attn.reshape(1, width),
        gain_mlp.reshape(1, width),
        w_query,
        w_key,
        w_value,
        w_out,
        w_in,
        w_down,
    )
    latent_end, trace, logp, total = pl.pallas_call(
        finish_kernel,
        out_shape=(
            jax.ShapeDtypeStruct((rows, width), F32),
            jax.ShapeDtypeStruct((1, rows), F32),
            jax.ShapeDtypeStruct((1, rows), F32),
            jax.ShapeDtypeStruct((1, 1), F32),
        ),
        in_specs=[vmem] * 3,
        out_specs=(vmem,) * 4,
    )(state, stats, mean)
    return (latent_end, trace.reshape(rows), logp.reshape(rows), total.reshape(()))


def solution(mesh):
    return jax.shard_map(
        functools.partial(per_device, mesh.shape["seq"], mesh.shape["head"]),
        mesh=mesh,
        in_specs=(
            P("seq", None),
            P("seq", None),
            P(),
            P(),
            P(None, "head"),
            P(None, "head"),
            P(None, "head"),
            P("head", None),
            P(),
            P(None, "head"),
            P("head", None),
        ),
        out_specs=(P("seq", None), P("seq"), P("seq"), P()),
        check_vma=False,
    )
```

time: 87.6 us -> 81 us (0.925)
  local copies, waits for them, and re-layouts: 4.34 us -> 0 us
  Pallas kernels: 82.3 us -> 80.2 us
    pallas_call x1, Pallas kernels: 82.3 us -> 78.3 us  [per_device(): pl.pallas_call(functools.partial(flow_kernel, n, m), out_shape=(jax.Shape...]
    unnamed x1 -> x0, local copies, waits for them, and re-layouts: 1.88 us -> none
    pallas_call x0 -> x1, Pallas kernels: none -> 1.88 us  [per_device(): pl.pallas_call(finish_kernel, out_shape=(jax.ShapeDtypeStruct((rows, widt...]
    squeeze x1 -> x0, local copies, waits for them, and re-layouts: 1.27 us -> none  [per_device(): return (state, stats[0], stats[1], mean[0, 0])]
    slice x1 -> x0, local copies, waits for them, and re-layouts: 1.19 us -> none  [per_device(): return (state, stats[0], stats[1], mean[0, 0])]
where the time goes in v2:
time: 81 us; the launch traced here: 80.8 us
  Pallas kernels  80.2 us (99%)
    pallas_call x1, Pallas kernels, per_device(): pl.pallas_call(functools.partial(flow_kernel, n, m), out_shape=(jax.Shape...  78.3 us
    pallas_call x1, Pallas kernels, per_device(): pl.pallas_call(finish_kernel, out_shape=(jax.ShapeDtypeStruct((rows, widt...  1.88 us

profile of v2, /device:TPU:0, one launch (start us, length us, event | category | flops | bytes accessed | tf_op | source)
XLA Modules:
  0.0 80.8 jit_solution(9761681744432562465)
XLA Ops:
  0.6 78.3 %shard_map.138 = (f32[128,1024]{1,0:T(8,128)}, f32[8,128]{1,0:T(8,128)}, f32[8,128]{1,0:T(8,128)}) custom-call(bf16[128,1024]{1,0:T(8,128)(2,1)} %latent.1, bf16[128,1024]{1,0:T(8,128)(2,1)} %probe.1, f32[1,1024]{1,0:T(1,128)} %bitcast.6, f32[1,1024]{1,0:T(1,128)} %bitcast.7, f32[1,1024]{1,0:T(1,128)} %bitcast.8, bf16[1024,256]{1,0:T(8,128)(2,1)} %w_query.1, ...), custom_call_target="tpu_custom_call" | custom-call | tf_op jit(solution)/shard_map/pallas_call | solution.py:811
  78.9 1.9 %shard_map.139 = (f32[128,1024]{1,0:T(8,128)}, f32[1,128]{1,0:T(1,128)}, f32[1,128]{1,0:T(1,128)}, f32[1,1]{1,0:T(1,128)}) custom-call(f32[128,1024]{1,0:T(8,128)} %get-tuple-element.11.state, f32[8,128]{1,0:T(8,128)} %get-tuple-element.12.stats, f32[8,128]{1,0:T(8,128)} %get-tuple-element.13.mean), custom_call_target="tpu_custom_call" | custom-call | tf_op jit(solution)/shard_map/pallas_call | solution.py:871
